TPU v7x, 32 devices: a whole 2x2x4 slice. The times are simulated.
32 devices in a mesh: dp: 4 (over y, x), centers: 8 (over z, core).
Axes of the slice: x: 2, y: 2, z: 4, core: 2. Of those that a mesh axis runs over, the one named last changes fastest.
Arguments:
- points: bfloat16 [16384, 32], P('dp'), may hold values from -6 to 6
- centers: bfloat16 [16384, 32], P('centers'), may hold values from -6 to 6
- coef: bfloat16 [16384, 64], P('centers'), may hold values from -0.1875 to 0.1875
Outputs:
- product: float32 [16384, 64], P('centers')
All inputs are finite; a program needn't handle non-finite values.
Results may differ from a plain program's by a relative error of at most 0.0003.
Values may be sent and summed in bfloat16 or wider, within the bound.
A program may use at most 128 MiB of HBM per device.

v0:
```python
import functools
import math

import jax
import jax.numpy as jnp
from jax import lax
from jax.experimental import pallas as pl
from jax.experimental.pallas import tpu as pltpu
from jax.sharding import PartitionSpec as P

MESH = pl.DeviceIdType.MESH
F32, BF16 = jnp.float32, jnp.bfloat16


def dot(a, b):
    return lax.dot_general(a, b, (((1,), (0,)), ((), ())), preferred_element_type=F32)


def dot_nt(a, b):
    return lax.dot_general(a, b, (((1,), (1,)), ((), ())), preferred_element_type=F32)


def split3(v):
    hi = v.astype(BF16).astype(F32)
    mid = (v - hi).astype(BF16).astype(F32)
    return hi, mid, (v - hi) - mid


def row_form(x, width):
    feats = x.shape[1]
    lane = lax.broadcasted_iota(jnp.int32, (feats, width), 1)
    sub = lax.broadcasted_iota(jnp.int32, (feats, width), 0)
    pick = ((lane % feats) == sub) & (lane < 3 * feats)
    spread = dot(x, pick.astype(F32).astype(BF16))
    wide = x.astype(F32)
    sq = jnp.sum(wide * wide, axis=1, keepdims=True) * (-2.0 * math.log2(math.e) / feats)
    hi, mid, lo = split3(sq)
    at = lax.broadcasted_iota(jnp.int32, (x.shape[0], width), 1) - 3 * feats
    tail = jnp.where(at == 3, hi, jnp.where(at == 4, mid, jnp.where(at == 5, lo, 0.0)))
    tail = jnp.where((at >= 0) & (at < 3), 1.0, tail)
    return (spread + tail).astype(BF16)


def col_form(ct, width):
    feats, count = ct.shape
    wide = ct.astype(F32)
    parts = [p.astype(BF16) for p in split3(wide * (4.0 * math.log2(math.e) / feats))]
    sq = jnp.sum(wide * wide, axis=0, keepdims=True) * (-2.0 * math.log2(math.e) / feats)
    hi, mid, lo = split3(sq)
    at = lax.broadcasted_iota(jnp.int32, (width - 3 * feats, count), 0)
    tail = jnp.where(at == 0, hi, jnp.where(at == 1, mid, jnp.where(at == 2, lo, 0.0)))
    tail = jnp.where((at >= 3) & (at < 6), 1.0, tail)
    return jnp.concatenate(parts + [tail.astype(BF16)], axis=0)


def kern(rows, cols):
    return jnp.exp2(dot(rows, cols)).astype(BF16)


def body(cfg, pts_hbm, cen_hbm, packed, out, pts, cen, lsem, sibp, kmat, colt, rowc, gath, reg, own_half, snd1, rcv1, snd2, rcv2,
         own_sum, fwd, csend, crecv, cown, full,
         as_, ar, fs, fr, b1s, b1r, b2s, b2r, gs, gr, hs, hr, cs, cr, ds_, dr):
    n_dp, n_c, feats, width = cfg
    n_h = n_c // 2
    d = lax.axis_index("dp")
    j = lax.axis_index("centers")
    par = lax.rem(j, 2)
    z = j // 2
    sib = j + 1 - 2 * par
    local_pts = pts.shape[0]
    local_cen = cen.shape[0]
    share = local_pts // n_c
    quarter = local_cen // n_dp
    step = min(1024, local_cen)
    alpha_scale = 1.0 / math.sqrt(local_pts * n_dp)

    def up(t):
        return lax.rem(z + 1 + t, n_h)

    def down(t):
        return lax.rem(z + 2 * n_h - 1 - t, n_h)

    def dup(t):
        return lax.rem(d + 1 + t, n_dp)

    def ddown(t):
        return lax.rem(d + 2 * n_dp - 1 - t, n_dp)

    def copy(src, dst, ssem, rsem, dev):
        return pltpu.make_async_remote_copy(
            src_ref=src, dst_ref=dst, send_sem=ssem, recv_sem=rsem, device_id=dev, device_id_type=MESH
        )

    barrier = pltpu.get_barrier_semaphore()
    for t in range(n_h - 1):
        pl.semaphore_signal(barrier, inc=1, device_id=(d, 2 * up(t) + par), device_id_type=MESH)
    pl.semaphore_signal(barrier, inc=1, device_id=(d, sib), device_id_type=MESH)
    for t in range(n_dp - 1):
        pl.semaphore_signal(barrier, inc=1, device_id=(dup(t), j), device_id_type=MESH)

    cen_in = pltpu.make_async_copy(cen_hbm, cen, lsem.at[0])
    pts_in = pltpu.make_async_copy(pts_hbm, pts, lsem.at[1])
    cen_in.start()
    pts_in.start()
    for c in range(local_cen // step):
        at = pl.ds(c * step, step)
        colt[:, at] = col_form(packed[:feats, at], width)
    cen_in.wait()
    for c in range(local_cen // step):
        at = pl.ds(c * step, step)
        rowc[at, :] = row_form(cen[at, :], width)
    reg[...] = jnp.zeros_like(reg)

    pl.semaphore_wait(barrier, n_h - 1 + 1 + n_dp - 1)

    mine = packed.at[:, pl.ds(pl.multiple_of(d * quarter, 128), quarter)]

    def gather(t):
        return copy(mine, gath.at[j], as_.at[t], ar.at[t], (d, 2 * up(t) + par))

    def gather_in(t):
        return copy(mine, gath.at[2 * down(t) + par], as_.at[t], ar.at[t], (d, 2 * up(t) + par))

    for t in range(n_h - 1):
        gather(t).start()
    own_to_sib = copy(packed, sibp, fs.at[n_h - 1], fr.at[n_h - 1], (d, sib))
    own_to_sib.start()
    pts_in.wait()

    def to_sib(t):
        return copy(snd1.at[t], rcv1.at[t], b1s.at[t], b1r.at[t], (d, sib))

    def to_peer(t):
        return copy(snd2.at[t], rcv2.at[t], b2s.at[t], b2r.at[t], (d, 2 * up(t) + par))

    def half(s):
        at = pl.ds(pl.multiple_of(s * share, share), share)
        rows = row_form(pts[at, :], width)
        acc = jnp.zeros((packed.shape[0] - feats, share), F32)
        for c in range(local_cen // step):
            cols = pl.ds(c * step, step)
            tile = kern(rows, colt[:, cols])
            kmat[at, cols] = tile
            acc = acc + dot_nt(packed[feats:, cols], tile)
        return acc

    @pl.loop(0, n_h)
    def _(t):
        zt = up(t)
        snd1[t] = half(2 * zt + 1 - par).astype(BF16)
        to_sib(t).start()
        own_half[...] = half(2 * zt + par)
        to_sib(t).wait_recv()
        total = own_half[...] + rcv1[t].astype(F32)

        @pl.when(t < n_h - 1)
        def _():
            snd2[t] = total.astype(BF16)
            to_peer(t).start()

        @pl.when(t == n_h - 1)
        def _():
            own_sum[...] = total

    def forward_block(t):
        at = gath.at[2 * down(t) + par]
        return copy(at, at, fs.at[t], fr.at[t], (d, sib))

    def forward_in(t):
        at = gath.at[2 * down(t) + 1 - par]
        return copy(at, at, fs.at[t], fr.at[t], (d, sib))

    for t in range(n_h - 1):
        gather_in(t).wait_recv()
        forward_block(t).start()

    def regular(block):
        cols = col_form(gath[block, :feats, :], width)
        weights = gath[block, feats:, :]
        for r in range(local_cen // step):
            rows = pl.ds(r * step, step)
            reg[:, rows] += dot_nt(weights, kern(rowc[rows, :], cols))

    for t in range(n_h - 1):
        to_peer(t).wait_recv()
    total = own_sum[...]
    for t in range(n_h - 1):
        total = total + rcv2[t].astype(F32)

    def slot(s):
        return fwd.at[:, pl.ds(pl.multiple_of(s * share, share), share)]

    def spread(t):
        return copy(slot(j), slot(j), gs.at[t], gr.at[t], (d, 2 * up(t) + par))

    def spread_in(t):
        at = slot(2 * down(t) + par)
        return copy(at, at, gs.at[t], gr.at[t], (d, 2 * up(t) + par))

    fwd[:, pl.ds(pl.multiple_of(j * share, share), share)] = total.astype(BF16)
    for t in range(n_h - 1):
        spread(t).start()
    own_fwd = copy(slot(j), slot(j), hs.at[n_h - 1], hr.at[n_h - 1], (d, sib))
    own_fwd.start()

    @pl.loop(0, n_h - 1)
    def _(i):
        regular(2 * up(i) + par)

    for t in range(n_h - 1):
        forward_in(t).wait_recv()

    cut = ((n_h - 1) * 2) // 3

    @pl.loop(0, cut)
    def _(i):
        regular(2 * up(i) + 1 - par)

    def relay(t):
        at = slot(2 * down(t) + par)
        return copy(at, at, hs.at[t], hr.at[t], (d, sib))

    def relay_in(t):
        at = slot(2 * down(t) + 1 - par)
        return copy(at, at, hs.at[t], hr.at[t], (d, sib))

    for t in range(n_h - 1):
        spread_in(t).wait_recv()
        relay(t).start()

    @pl.loop(cut, n_h - 1)
    def _(i):
        regular(2 * up(i) + 1 - par)

    for t in range(n_h - 1):
        relay_in(t).wait_recv()
    copy(slot(sib), slot(sib), hs.at[n_h - 1], hr.at[n_h - 1], (d, sib)).wait_recv()

    def cross(t):
        return copy(csend.at[t], crecv.at[t], cs.at[t], cr.at[t], (dup(t), j))

    @pl.loop(0, n_dp)
    def _(t):
        at = pl.ds(pl.multiple_of(dup(t) * quarter, 128), quarter)
        back = dot(fwd[...], kmat[:, at]) * alpha_scale + reg[:, at]

        @pl.when(t < n_dp - 1)
        def _():
            csend[t] = back
            cross(t).start()

        @pl.when(t == n_dp - 1)
        def _():
            cown[...] = back

    own_to_sib.wait_recv()
    mine_rows = rowc[pl.ds(pl.multiple_of(d * quarter, 128), quarter), :]
    for c in range(local_cen // step):
        at = pl.ds(c * step, step)
        cown[...] += dot_nt(packed[feats:, at], kern(mine_rows, colt[:, at]))
        cown[...] += dot_nt(sibp[feats:, at], kern(mine_rows, col_form(sibp[:feats, at], width)))

    for t in range(n_dp - 1):
        cross(t).wait_recv()
    total = cown[...]
    for t in range(n_dp - 1):
        total = total + crecv[t]
    full[d] = total

    def publish(t):
        return copy(full.at[d], full.at[d], ds_.at[t], dr.at[t], (dup(t), j))

    def publish_in(t):
        at = full.at[ddown(t)]
        return copy(at, at, ds_.at[t], dr.at[t], (dup(t), j))

    for t in range(n_dp - 1):
        publish(t).start()
    for t in range(n_h - 1):
        gather(t).wait_send()
        forward_block(t).wait_send()
        to_peer(t).wait_send()
        spread(t).wait_send()
        relay(t).wait_send()
    for t in range(n_h):
        to_sib(t).wait_send()
    own_to_sib.wait_send()
    own_fwd.wait_send()
    for t in range(n_dp - 1):
        cross(t).wait_send()
    for t in range(n_dp - 1):
        publish_in(t).wait_recv()
    for t in range(n_dp - 1):
        publish(t).wait_send()
    for q in range(n_dp):
        out[:, q * quarter:(q + 1) * quarter] = full[q]


def solution(mesh):
    n_dp, n_c = mesh.shape["dp"], mesh.shape["centers"]

    def on_device(points, centers, coef):
        local_pts, feats = points.shape
        local_cen, outs = coef.shape
        width = -(-(3 * feats + 6) // 128) * 128
        n_h = n_c // 2
        share, quarter = local_pts // n_c, local_cen // n_dp
        packed = jnp.concatenate([centers, coef], axis=1).T
        dma = pltpu.SemaphoreType.DMA
        result = pl.pallas_call(
            functools.partial(body, (n_dp, n_c, feats, width)),
            out_shape=jax.ShapeDtypeStruct((outs, local_cen), F32),
            in_specs=[pl.BlockSpec(memory_space=pl.ANY)] * 2 + [pl.BlockSpec(memory_space=pltpu.VMEM)],
            out_specs=pl.BlockSpec(memory_space=pltpu.VMEM),
            scratch_shapes=[
                pltpu.VMEM((local_pts, feats), BF16),
                pltpu.VMEM((local_cen, feats), BF16),
                dma((2,)),
                pltpu.VMEM((feats + outs, local_cen), BF16),
                pltpu.VMEM((local_pts, local_cen), BF16),
                pltpu.VMEM((width, local_cen), BF16),
                pltpu.VMEM((local_cen, width), BF16),
                pltpu.VMEM((n_c, feats + outs, quarter), BF16),
                pltpu.VMEM((outs, local_cen), F32),
                pltpu.VMEM((outs, share), F32),
                pltpu.VMEM((n_h, outs, share), BF16),
                pltpu.VMEM((n_h, outs, share), BF16),
                pltpu.VMEM((n_h, outs, share), BF16),
                pltpu.VMEM((n_h, outs, share), BF16),
                pltpu.VMEM((outs, share), F32),
                pltpu.VMEM((outs, local_pts), BF16),
                pltpu.VMEM((n_dp, outs, quarter), F32),
                pltpu.VMEM((n_dp, outs, quarter), F32),
                pltpu.VMEM((outs, quarter), F32),
                pltpu.VMEM((n_dp, outs, quarter), F32),
            ] + [dma((n_h,))] * 12 + [dma((n_dp,))] * 4,
            compiler_params=pltpu.CompilerParams(
                collective_id=0, has_side_effects=True, vmem_limit_bytes=60 * 1024 * 1024
            ),
        )(points, centers, packed)
        return result.T

    return jax.shard_map(
        on_device,
        mesh=mesh,
        in_specs=(P("dp", None), P("centers", None), P("centers", None)),
        out_specs=P("centers", None),
        check_vma=False,
    )
```

profile of v0, /device:TPU:0, one launch (start us, length us, event | category | flops | bytes accessed | tf_op | source)
XLA Modules:
  0.0 53.3 jit_solution(6235959549221851688)
XLA Ops:
  0.0 0.0 copy-start
  0.0 1.8 %maximum_bitcast_fusion.packed = bf16[96,2048]{1,0:T(8,128)(2,1)} fusion(bf16[2048,64]{0,1:T(8,128)(2,1)} %param.5, bf16[2048,32]{0,1:T(8,128)(2,1)} %param.4), kind=kLoop, calls=%fused_computation | loop fusion | flops 786432 | bytes 786432 | tf_op jit(solution)/shard_map/transpose | solution.py:308
  1.8 0.0 copy-done
  1.8 0.0 copy-start.1
  1.8 1.0 %copy.5.cen_hbm = bf16[2048,32]{1,0:T(8,128)(2,1)} copy(bf16[2048,32]{0,1:T(8,128)(2,1)S(1)} %copy-done) | data formatting | bytes 262144 | tf_op args[1]
  2.8 0.0 copy-done.1
  2.8 1.3 %copy.4.pts_hbm = bf16[4096,32]{1,0:T(8,128)(2,1)} copy(bf16[4096,32]{0,1:T(8,128)(2,1)S(1)} %copy-done.1) | data formatting | bytes 524288 | tf_op args[0]
  4.1 47.3 %shard_map.37 = f32[64,2048]{1,0:T(8,128)} custom-call(bf16[4096,32]{1,0:T(8,128)(2,1)} %copy.4.pts_hbm, bf16[2048,32]{1,0:T(8,128)(2,1)} %copy.5.cen_hbm, bf16[96,2048]{1,0:T(8,128)(2,1)} %maximum_bitcast_fusion.packed), custom_call_target="tpu_custom_call" | custom-call | tf_op jit(solution)/shard_map/pallas_call | solution.py:310
  51.4 1.9 %copy.7 = f32[2048,64]{0,1:T(8,128)} copy(f32[2048,64]{0,1:T(8,128)} %bitcast.3) | data formatting | bytes 1048576
Async XLA Ops:
  0.0 1.8 %copy-start = (bf16[2048,32]{0,1:T(8,128)(2,1)S(1)}, bf16[2048,32]{0,1:T(8,128)(2,1)}, u32[]{:S(2)}) copy-start(bf16[2048,32]{0,1:T(8,128)(2,1)} %param.4) | copy-start | bytes 393220
  1.8 1.0 %copy-start.1 = (bf16[4096,32]{0,1:T(8,128)(2,1)S(1)}, bf16[4096,32]{0,1:T(8,128)(2,1)}, u32[]{:S(2)}) copy-start(bf16[4096,32]{0,1:T(8,128)(2,1)} %param.3) | copy-start | bytes 786436
where the time goes:
time: 53.6 us; the launch traced here: 53.3 us
  Pallas kernels  47.3 us (88%)
  local copies, waits for them, and re-layouts  4.2 us (8%)
  other arithmetic  1.79 us (3%)
    pallas_call x1, Pallas kernels, on_device(): pl.pallas_call(functools.partial(body, (n_dp, n_c, feats, width)), out_sh...  47.3 us
    unnamed x7, local copies, waits for them, and re-layouts  4.2 us
    transpose x1, other arithmetic, on_device(): packed = jnp.concatenate([centers, coef], axis=1).T  1.79 us

commit v1 on v0

--- a/solution.py
+++ b/solution.py
@@ -26,19 +26,15 @@
     return hi, mid, (v - hi) - mid
 
 
-def row_form(x, width):
-    feats = x.shape[1]
-    lane = lax.broadcasted_iota(jnp.int32, (feats, width), 1)
-    sub = lax.broadcasted_iota(jnp.int32, (feats, width), 0)
-    pick = ((lane % feats) == sub) & (lane < 3 * feats)
-    spread = dot(x, pick.astype(F32).astype(BF16))
-    wide = x.astype(F32)
-    sq = jnp.sum(wide * wide, axis=1, keepdims=True) * (-2.0 * math.log2(math.e) / feats)
+def row_form(xt, width):
+    feats, count = xt.shape
+    wide = xt.astype(F32)
+    sq = jnp.sum(wide * wide, axis=0, keepdims=True) * (-2.0 * math.log2(math.e) / feats)
     hi, mid, lo = split3(sq)
-    at = lax.broadcasted_iota(jnp.int32, (x.shape[0], width), 1) - 3 * feats
+    at = lax.broadcasted_iota(jnp.int32, (width - 3 * feats, count), 0)
     tail = jnp.where(at == 3, hi, jnp.where(at == 4, mid, jnp.where(at == 5, lo, 0.0)))
-    tail = jnp.where((at >= 0) & (at < 3), 1.0, tail)
-    return (spread + tail).astype(BF16)
+    tail = jnp.where(at < 3, 1.0, tail)
+    return jnp.concatenate([xt, xt, xt, tail.astype(BF16)], axis=0).T
 
 
 def col_form(ct, width):
@@ -57,7 +53,7 @@
     return jnp.exp2(dot(rows, cols)).astype(BF16)
 
 
-def body(cfg, pts_hbm, cen_hbm, packed, out, pts, cen, lsem, sibp, kmat, colt, rowc, gath, reg, own_half, snd1, rcv1, snd2, rcv2,
+def body(cfg, pts_hbm, cen_hbm, coef_hbm, out, pts, packed, lsem, sibp, kmat, colt, rowc, gath, reg, own_half, snd1, rcv1, snd2, rcv2,
          own_sum, fwd, csend, crecv, cown, full,
          as_, ar, fs, fr, b1s, b1r, b2s, b2r, gs, gr, hs, hr, cs, cr, ds_, dr):
     n_dp, n_c, feats, width = cfg
@@ -67,8 +63,8 @@
     par = lax.rem(j, 2)
     z = j // 2
     sib = j + 1 - 2 * par
-    local_pts = pts.shape[0]
-    local_cen = cen.shape[0]
+    local_pts = pts.shape[1]
+    local_cen = packed.shape[1]
     share = local_pts // n_c
     quarter = local_cen // n_dp
     step = min(1024, local_cen)
@@ -98,20 +94,23 @@
     for t in range(n_dp - 1):
         pl.semaphore_signal(barrier, inc=1, device_id=(dup(t), j), device_id_type=MESH)
 
-    cen_in = pltpu.make_async_copy(cen_hbm, cen, lsem.at[0])
-    pts_in = pltpu.make_async_copy(pts_hbm, pts, lsem.at[1])
+    cen_in = pltpu.make_async_copy(cen_hbm, packed.at[:feats], lsem.at[0])
+    coef_in = pltpu.make_async_copy(coef_hbm, packed.at[feats:], lsem.at[1])
+    pts_in = pltpu.make_async_copy(pts_hbm, pts, lsem.at[2])
     cen_in.start()
+    coef_in.start()
     pts_in.start()
+    cen_in.wait()
     for c in range(local_cen // step):
         at = pl.ds(c * step, step)
         colt[:, at] = col_form(packed[:feats, at], width)
-    cen_in.wait()
     for c in range(local_cen // step):
         at = pl.ds(c * step, step)
-        rowc[at, :] = row_form(cen[at, :], width)
+        rowc[at, :] = row_form(packed[:feats, at], width)
     reg[...] = jnp.zeros_like(reg)
 
     pl.semaphore_wait(barrier, n_h - 1 + 1 + n_dp - 1)
+    coef_in.wait()
 
     mine = packed.at[:, pl.ds(pl.multiple_of(d * quarter, 128), quarter)]
 
@@ -135,7 +134,7 @@
 
     def half(s):
         at = pl.ds(pl.multiple_of(s * share, share), share)
-        rows = row_form(pts[at, :], width)
+        rows = row_form(pts[:, at], width)
         acc = jnp.zeros((packed.shape[0] - feats, share), F32)
         for c in range(local_cen // step):
             cols = pl.ds(c * step, step)
@@ -305,17 +304,16 @@
         width = -(-(3 * feats + 6) // 128) * 128
         n_h = n_c // 2
         share, quarter = local_pts // n_c, local_cen // n_dp
-        packed = jnp.concatenate([centers, coef], axis=1).T
         dma = pltpu.SemaphoreType.DMA
         result = pl.pallas_call(
             functools.partial(body, (n_dp, n_c, feats, width)),
             out_shape=jax.ShapeDtypeStruct((outs, local_cen), F32),
-            in_specs=[pl.BlockSpec(memory_space=pl.ANY)] * 2 + [pl.BlockSpec(memory_space=pltpu.VMEM)],
+            in_specs=[pl.BlockSpec(memory_space=pl.ANY)] * 3,
             out_specs=pl.BlockSpec(memory_space=pltpu.VMEM),
             scratch_shapes=[
-                pltpu.VMEM((local_pts, feats), BF16),
-                pltpu.VMEM((local_cen, feats), BF16),
-                dma((2,)),
+                pltpu.VMEM((feats, local_pts), BF16),
+                pltpu.VMEM((feats + outs, local_cen), BF16),
+                dma((3,)),
                 pltpu.VMEM((feats + outs, local_cen), BF16),
                 pltpu.VMEM((local_pts, local_cen), BF16),
                 pltpu.VMEM((width, local_cen), BF16),
@@ -337,7 +335,7 @@
             compiler_params=pltpu.CompilerParams(
                 collective_id=0, has_side_effects=True, vmem_limit_bytes=60 * 1024 * 1024
             ),
-        )(points, centers, packed)
+        )(points.T, centers.T, coef.T)
         return result.T
 
     return jax.shard_map(

time: 53.6 us -> 47.9 us (0.89)
  local copies, waits for them, and re-layouts: 4.2 us -> 1.87 us
  other arithmetic: 1.79 us -> 0 us
  Pallas kernels: 47.3 us -> 45.8 us
    unnamed x7 -> x1, local copies, waits for them, and re-layouts: 4.2 us -> 1.87 us
    transpose x1 -> x0, other arithmetic: 1.79 us -> none  [on_device(): packed = jnp.concatenate([centers, coef], axis=1).T]
    pallas_call x1, Pallas kernels: 47.3 us -> 45.8 us  [on_device(): pl.pallas_call(functools.partial(body, (n_dp, n_c, feats, width)), out_sh...]
where the time goes in v1:
time: 47.9 us; the launch traced here: 47.7 us
  Pallas kernels  45.8 us (96%)
  local copies, waits for them, and re-layouts  1.87 us (4%)
    pallas_call x1, Pallas kernels, on_device(): pl.pallas_call(functools.partial(body, (n_dp, n_c, feats, width)), out_sh...  45.8 us
    unnamed x1, local copies, waits for them, and re-layouts  1.87 us

profile of v1, /device:TPU:0, one launch (start us, length us, event | category | flops | bytes accessed | tf_op | source)
XLA Modules:
  0.0 47.7 jit_solution(11584640358321465687)
XLA Ops:
  0.0 45.8 %shard_map.37 = f32[64,2048]{1,0:T(8,128)} custom-call(bf16[32,4096]{1,0:T(8,128)(2,1)} %bitcast.5, bf16[32,2048]{1,0:T(8,128)(2,1)} %bitcast.7, bf16[64,2048]{1,0:T(8,128)(2,1)} %bitcast.6), custom_call_target="tpu_custom_call" | custom-call | tf_op jit(solution)/shard_map/pallas_call | solution.py:308
  45.8 1.9 %copy.5 = f32[2048,64]{0,1:T(8,128)} copy(f32[2048,64]{0,1:T(8,128)} %bitcast.4) | data formatting | bytes 1048576

commit v2 on v1

v2 whole, which is shorter than its diff:
```python
import functools
import math

import jax
import jax.numpy as jnp
from jax import lax
from jax.experimental import pallas as pl
from jax.experimental.pallas import tpu as pltpu
from jax.sharding import PartitionSpec as P

MESH = pl.DeviceIdType.MESH
F32, BF16 = jnp.float32, jnp.bfloat16
PIECE = 512


def dot(a, b):
    return lax.dot_general(a, b, (((1,), (0,)), ((), ())), preferred_element_type=F32)


def dot_nt(a, b):
    return lax.dot_general(a, b, (((1,), (1,)), ((), ())), preferred_element_type=F32)


def split3(v):
    hi = v.astype(BF16).astype(F32)
    mid = (v - hi).astype(BF16).astype(F32)
    return hi, mid, (v - hi) - mid


def row_form(xt, width):
    feats, count = xt.shape
    wide = xt.astype(F32)
    sq = jnp.sum(wide * wide, axis=0, keepdims=True) * (-2.0 * math.log2(math.e) / feats)
    hi, mid, lo = split3(sq)
    at = lax.broadcasted_iota(jnp.int32, (width - 3 * feats, count), 0)
    tail = jnp.where(at == 3, hi, jnp.where(at == 4, mid, jnp.where(at == 5, lo, 0.0)))
    tail = jnp.where(at < 3, 1.0, tail)
    return jnp.concatenate([xt, xt, xt, tail.astype(BF16)], axis=0).T


def col_form(ct, width):
    feats, count = ct.shape
    wide = ct.astype(F32)
    parts = [p.astype(BF16) for p in split3(wide * (4.0 * math.log2(math.e) / feats))]
    sq = jnp.sum(wide * wide, axis=0, keepdims=True) * (-2.0 * math.log2(math.e) / feats)
    hi, mid, lo = split3(sq)
    at = lax.broadcasted_iota(jnp.int32, (width - 3 * feats, count), 0)
    tail = jnp.where(at == 0, hi, jnp.where(at == 1, mid, jnp.where(at == 2, lo, 0.0)))
    tail = jnp.where((at >= 3) & (at < 6), 1.0, tail)
    return jnp.concatenate(parts + [tail.astype(BF16)], axis=0)


def xor(v, k):
    out, bit = v, 1
    while bit <= k:
        if k & bit:
            out = out + bit - 2 * bit * lax.rem(v // bit, 2)
        bit *= 2
    return out


def staggered(pieces, lag=1):
    held = []
    for logits, apply in pieces:
        e = logits()
        if len(held) == lag:
            tile, use = held.pop(0)
            use(tile)
        held.append((jnp.exp2(e).astype(BF16), apply))
    for tile, use in held:
        use(tile)


def body(cfg, pts_hbm, cen_hbm, coef_hbm, out, pts, packed, lsem, sibp, kmat, colt, gath, reg, own_half, snd1, rcv1, snd2, rcv2,
         own_sum, fwd, csend, crecv, cown, full, rowp, loc,
         os_, or_, b1s, b1r, b2s, b2r, gs, gr, hs, hr, ups, upr, dns, dnr, fus, fur, fds, fdr, cs, cr, ds_, dr):
    n_dp, n_c, feats, width, n_ck, n_cc = cfg
    n_h = n_c // 2
    d = lax.axis_index("dp")
    j = lax.axis_index("centers")
    par = lax.rem(j, 2)
    z = j // 2
    sib = j + 1 - 2 * par
    local_pts = pts.shape[1]
    local_cen = packed.shape[1]
    outs = packed.shape[0] - feats
    share = local_pts // n_c
    sh = share // n_ck
    span = n_c * sh
    quarter = local_cen // n_dp
    cw = quarter // n_cc
    piece = min(PIECE, local_cen)
    alpha_scale = 1.0 / math.sqrt(local_pts * n_dp)

    def copy(src, dst, ssem, rsem, dev):
        return pltpu.make_async_remote_copy(
            src_ref=src, dst_ref=dst, send_sem=ssem, recv_sem=rsem, device_id=dev, device_id_type=MESH
        )

    def peer(k):
        return (d, 2 * xor(z, k) + par)

    barrier = pltpu.get_barrier_semaphore()
    for k in range(1, n_h):
        pl.semaphore_signal(barrier, inc=1, device_id=peer(k), device_id_type=MESH)
    pl.semaphore_signal(barrier, inc=1, device_id=(d, sib), device_id_type=MESH)
    for k in range(1, n_dp):
        pl.semaphore_signal(barrier, inc=1, device_id=(xor(d, k), j), device_id_type=MESH)

    cen_in = pltpu.make_async_copy(cen_hbm, packed.at[:feats], lsem.at[0])
    coef_in = pltpu.make_async_copy(coef_hbm, packed.at[feats:], lsem.at[1])
    pts_in = pltpu.make_async_copy(pts_hbm, pts, lsem.at[2])
    cen_in.start()
    coef_in.start()
    pts_in.start()
    cen_in.wait()
    for c in range(local_cen // piece):
        at = pl.ds(c * piece, piece)
        colt[:, at] = col_form(packed[:feats, at], width)
    reg[...] = jnp.zeros_like(reg)
    loc[...] = jnp.zeros_like(loc)
    coef_in.wait()
    pts_in.wait()

    mine = packed.at[:, pl.ds(pl.multiple_of(d * quarter, 128), quarter)]

    def up(r):
        dst = gath.at[2 * (z - r) + par]
        return copy(mine if r == 0 else dst, dst, ups.at[r], upr.at[r], (d, 2 * (z + 1) + par))

    def down(r):
        dst = gath.at[2 * (z + r) + par]
        return copy(mine if r == 0 else dst, dst, dns.at[r], dnr.at[r], (d, 2 * (z - 1) + par))

    def up_in(r):
        dst = gath.at[2 * (z - r) + par]
        return copy(dst, dst, ups.at[r - 1], upr.at[r - 1], (d, sib))

    def down_in(r):
        dst = gath.at[2 * (z + r) + par]
        return copy(dst, dst, dns.at[r - 1], dnr.at[r - 1], (d, sib))

    def below_sib(r):
        at = gath.at[2 * (z - r) + par]
        return copy(at, at, fus.at[r], fur.at[r], (d, sib))

    def above_sib(r):
        at = gath.at[2 * (z + r) + par]
        return copy(at, at, fds.at[r], fdr.at[r], (d, sib))

    def below_sib_in(r):
        at = gath.at[2 * (z - r) + 1 - par]
        return copy(at, at, fus.at[r], fur.at[r], (d, sib))

    def above_sib_in(r):
        at = gath.at[2 * (z + r) + 1 - par]
        return copy(at, at, fds.at[r], fdr.at[r], (d, sib))

    def hop(r):
        if r > 0:
            @pl.when(z >= r)
            def _():
                up_in(r).wait_recv()
                below_sib(r).start()

            @pl.when(z + r < n_h)
            def _():
                down_in(r).wait_recv()
                above_sib(r).start()

        if r < n_h - 1:
            @pl.when((z >= r) & (z < n_h - 1))
            def _():
                up(r).start()

            @pl.when((z + r < n_h) & (z > 0))
            def _():
                down(r).start()

    def hop_sib_in(r):
        @pl.when(z >= r)
        def _():
            below_sib_in(r).wait_recv()

        @pl.when(z + r < n_h)
        def _():
            above_sib_in(r).wait_recv()

    def hop_sent(r):
        if r > 0:
            @pl.when(z >= r)
            def _():
                below_sib(r).wait_send()

            @pl.when(z + r < n_h)
            def _():
                above_sib(r).wait_send()

        if r < n_h - 1:
            @pl.when((z >= r) & (z < n_h - 1))
            def _():
                up(r).wait_send()

            @pl.when((z + r < n_h) & (z > 0))
            def _():
                down(r).wait_send()

    own_to_sib = copy(packed, sibp, os_.at[0], or_.at[0], (d, sib))

    def to_sib(s):
        return copy(snd1.at[s], rcv1.at[s], b1s.at[s], b1r.at[s], (d, sib))

    def to_peer(c, k):
        i = c * n_h + k
        return copy(snd2.at[i], rcv2.at[i], b2s.at[i], b2r.at[i], peer(k))

    def slot(c, q):
        return fwd.at[:, pl.ds(pl.multiple_of(c * span + q * sh, sh), sh)]

    def spread(c, k):
        i = c * n_h + k
        return copy(slot(c, j), slot(c, j), gs.at[i], gr.at[i], peer(k))

    def spread_in(c, k):
        i = c * n_h + k
        at = slot(c, 2 * xor(z, k) + par)
        return copy(at, at, gs.at[i], gr.at[i], peer(k))

    def relay(c, k):
        i = c * n_h + k
        at = slot(c, 2 * xor(z, k) + par)
        return copy(at, at, hs.at[i], hr.at[i], (d, sib))

    def relay_in(c, k):
        i = c * n_h + k
        at = slot(c, 2 * xor(z, k) + 1 - par)
        return copy(at, at, hs.at[i], hr.at[i], (d, sib))

    steps = n_ck * n_h

    group = 2

    def owners(s):
        zt = xor(z, n_h - 1 - s % n_h)
        return 2 * zt + 1 - par, 2 * zt + par

    def point_rows(g):
        for i, s in enumerate(range(g * group, (g + 1) * group)):
            for h, q in enumerate(owners(s)):
                src = pl.ds(pl.multiple_of(q * share + (s // n_h) * sh, sh), sh)
                rowp[g % 2, i, h * sh:(h + 1) * sh, :] = row_form(pts[:, src], width)

    def forward(g):
        if (g + 1) * group < steps:
            point_rows(g + 1)
        pieces = []
        accs = []
        for i, s in enumerate(range(g * group, (g + 1) * group)):
            acc = [jnp.zeros((outs, 2 * sh), F32)]
            accs.append(acc)
            ats = [pl.ds(pl.multiple_of((s // n_h) * span + q * sh, sh), sh) for q in owners(s)]
            for b in range(local_cen // piece):
                cols = pl.ds(b * piece, piece)

                def logits(i=i, cols=cols):
                    return dot(rowp[g % 2, i], colt[:, cols])

                def apply(tile, acc=acc, ats=ats, cols=cols):
                    for h in range(2):
                        kmat[ats[h], cols] = tile[h * sh:(h + 1) * sh]
                    acc[0] = acc[0] + dot_nt(packed[feats:, cols], tile)

                pieces.append((logits, apply))
        staggered(pieces)
        for acc, s in zip(accs, range(g * group, (g + 1) * group)):
            snd1[s] = acc[0][:, :sh].astype(BF16)
            own_half[s] = acc[0][:, sh:]

    def combine(s):
        c, k = s // n_h, n_h - 1 - s % n_h
        to_sib(s).wait_recv()
        total = own_half[s] + rcv1[s].astype(F32)
        if k > 0:
            snd2[c * n_h + k] = total.astype(BF16)
            to_peer(c, k).start()
        else:
            own_sum[c] = total

    def finish(c):
        for k in range(1, n_h):
            to_peer(c, k).wait_recv()
        total = own_sum[c]
        for k in range(1, n_h):
            total = total + rcv2[c * n_h + k].astype(F32)
        slot(c, j)[...] = total.astype(BF16)
        for k in reversed(range(1, n_h)):
            spread(c, k).start()
        relay(c, 0).start()

    def relays(c):
        for k in range(1, n_h):
            spread_in(c, k).wait_recv()
            relay(c, k).start()

    def regular(*blocks):
        pieces = []
        for block in blocks:
            rows = row_form(gath[block, :feats, :], width)
            weights = gath[block, feats:, :]
            for r in range(0, quarter, 256):
                part = slice(r, r + 256)
                for b in range(local_cen // piece):
                    cols = pl.ds(b * piece, piece)

                    def logits(rows=rows[part], cols=cols):
                        return dot(rows, colt[:, cols])

                    def apply(tile, weights=weights[:, part], cols=cols):
                        reg[:, cols] += dot(weights, tile)

                    pieces.append((logits, apply))
        staggered(pieces, 2)

    def back(c, at):
        rows = pl.ds(c * span, span)
        return dot(fwd[:, rows], kmat[rows, at]) * alpha_scale

    hops = list(range(1, n_h))
    sib_hops = list(range(1, n_h))

    def ensure(r):
        while hops and hops[0] <= r:
            hop(hops.pop(0))

    def ensure_sib(r):
        ensure(r)
        while sib_hops and sib_hops[0] <= r:
            hop_sib_in(sib_hops.pop(0))

    own_cols = pl.ds(pl.multiple_of(d * quarter, 128), quarter)

    def local(src):
        total = [loc[...]]
        pieces = []
        for b in range(local_cen // piece):
            at = pl.ds(b * piece, piece)

            def logits(at=at):
                return dot(row_form(src[:feats, at], width), colt[:, own_cols])

            def apply(tile, at=at):
                total[0] = total[0] + dot(src[feats:, at], tile)

            pieces.append((logits, apply))
        staggered(pieces)
        loc[...] = total[0]

    last = n_ck - 1
    groups = steps // group
    point_rows(0)
    for g in range(groups):
        forward(g)
        if g == 0:
            pl.semaphore_wait(barrier, n_h - 1 + 1 + n_dp - 1)
        for s in range(g * group, (g + 1) * group):
            to_sib(s).start()
        if g == 0:
            hop(0)
        if g > 0:
            for s in range((g - 1) * group, g * group):
                combine(s)
        if g == groups - 2:
            ensure(1)
            own_to_sib.start()
    near = 2 * xor(z, 1)
    ensure_sib(1)
    regular(near + par)
    for s in range(steps - group, steps):
        combine(s)
    if n_ck > 1:
        finish(0)
    regular(near + 1 - par)
    local(packed)
    ensure(2)
    finish(last)
    own_to_sib.wait_recv()
    local(sibp)
    rest = list(range(2, n_h))
    for k in rest[:-1]:
        ensure(k)
        regular(2 * xor(z, k) + par)
        ensure_sib(k)
        regular(2 * xor(z, k) + 1 - par)
    if n_ck > 1:
        relays(0)
        for k in range(n_h):
            relay_in(0, k).wait_recv()
        for b in range(local_cen // piece):
            cols = pl.ds(b * piece, piece)
            reg[:, cols] += back(0, cols)
    for k in rest[-1:]:
        ensure(k)
        relays(last)
        ensure_sib(k)
        regular(2 * xor(z, k) + par, 2 * xor(z, k) + 1 - par)
    if not rest:
        relays(last)
    for k in range(n_h):
        relay_in(last, k).wait_recv()

    def cross(cc, k):
        i = cc * n_dp + k
        return copy(csend.at[i], crecv.at[i], cs.at[i], cr.at[i], (xor(d, k), j))

    for cc in range(n_cc):
        for k in reversed(range(n_dp)):
            at = pl.ds(pl.multiple_of(xor(d, k) * quarter + cc * cw, 128), cw)
            total = back(last, at) + reg[:, at]
            if k > 0:
                csend[cc * n_dp + k] = total
            else:
                cown[cc] = total + loc[:, cc * cw:(cc + 1) * cw]
        for k in reversed(range(1, n_dp)):
            cross(cc, k).start()

    def publish(cc, k):
        i = cc * n_dp + k
        at = full.at[cc, d]
        return copy(at, at, ds_.at[i], dr.at[i], (xor(d, k), j))

    def publish_in(cc, k):
        i = cc * n_dp + k
        at = full.at[cc, xor(d, k)]
        return copy(at, at, ds_.at[i], dr.at[i], (xor(d, k), j))

    for cc in range(n_cc):
        for k in range(1, n_dp):
            cross(cc, k).wait_recv()
        total = cown[cc]
        for k in range(1, n_dp):
            total = total + crecv[cc * n_dp + k]
        full[cc, d] = total
        for k in reversed(range(1, n_dp)):
            publish(cc, k).start()

    for r in range(n_h):
        hop_sent(r)
    for s in range(steps):
        to_sib(s).wait_send()
    own_to_sib.wait_send()
    for c in range(n_ck):
        relay(c, 0).wait_send()
        for k in range(1, n_h):
            to_peer(c, k).wait_send()
            spread(c, k).wait_send()
            relay(c, k).wait_send()
    for cc in range(n_cc):
        for k in range(1, n_dp):
            cross(cc, k).wait_send()
            publish_in(cc, k).wait_recv()
        for q in range(n_dp):
            out[:, q * quarter + cc * cw:q * quarter + (cc + 1) * cw] = full[cc, q]
    for cc in range(n_cc):
        for k in range(1, n_dp):
            publish(cc, k).wait_send()


def solution(mesh):
    n_dp, n_c = mesh.shape["dp"], mesh.shape["centers"]

    def on_device(points, centers, coef):
        local_pts, feats = points.shape
        local_cen, outs = coef.shape
        width = -(-(3 * feats + 6) // 128) * 128
        n_h = n_c // 2
        share, quarter = local_pts // n_c, local_cen // n_dp
        n_ck = 2 if share % 256 == 0 else 1
        n_cc = 2 if quarter % 256 == 0 else 1
        sh, cw = share // n_ck, quarter // n_cc
        dma = pltpu.SemaphoreType.DMA
        args = [pltpu.with_memory_space_constraint(v.T, pltpu.HBM) for v in (points, centers, coef)]
        result = pl.pallas_call(
            functools.partial(body, (n_dp, n_c, feats, width, n_ck, n_cc)),
            out_shape=jax.ShapeDtypeStruct((outs, local_cen), F32),
            in_specs=[pl.BlockSpec(memory_space=pl.ANY)] * 3,
            out_specs=pl.BlockSpec(memory_space=pltpu.VMEM),
            scratch_shapes=[
                pltpu.VMEM((feats, local_pts), BF16),
                pltpu.VMEM((feats + outs, local_cen), BF16),
                dma((3,)),
                pltpu.VMEM((feats + outs, local_cen), BF16),
                pltpu.VMEM((local_pts, local_cen), BF16),
                pltpu.VMEM((width, local_cen), BF16),
                pltpu.VMEM((n_c, feats + outs, quarter), BF16),
                pltpu.VMEM((outs, local_cen), F32),
                pltpu.VMEM((n_ck * n_h, outs, sh), F32),
                pltpu.VMEM((n_ck * n_h, outs, sh), BF16),
                pltpu.VMEM((n_ck * n_h, outs, sh), BF16),
                pltpu.VMEM((n_ck * n_h, outs, sh), BF16),
                pltpu.VMEM((n_ck * n_h, outs, sh), BF16),
                pltpu.VMEM((n_ck, outs, sh), F32),
                pltpu.VMEM((outs, local_pts), BF16),
                pltpu.VMEM((n_cc * n_dp, outs, cw), F32),
                pltpu.VMEM((n_cc * n_dp, outs, cw), F32),
                pltpu.VMEM((n_cc, outs, cw), F32),
                pltpu.VMEM((n_cc, n_dp, outs, cw), F32),
                pltpu.VMEM((2, 2, 2 * sh, width), BF16),
                pltpu.VMEM((outs, quarter), F32),
            ] + [dma((1,))] * 2 + [dma((n_ck * n_h,))] * 8 + [dma((n_h,))] * 8 + [dma((n_cc * n_dp,))] * 4,
            compiler_params=pltpu.CompilerParams(
                collective_id=0, has_side_effects=True, vmem_limit_bytes=40 * 1024 * 1024
            ),
        )(*args)
        return result.T

    return jax.shard_map(
        on_device,
        mesh=mesh,
        in_specs=(P("dp", None), P("centers", None), P("centers", None)),
        out_specs=P("centers", None),
        check_vma=False,
    )
```

time: 47.9 us -> 44.7 us (0.933)
  Pallas kernels: 45.8 us -> 43.7 us
  local copies, waits for them, and re-layouts: 1.87 us -> 0.8 us
    pallas_call x1, Pallas kernels: 45.8 us -> 43.7 us  [on_device(): pl.pallas_call(functools.partial(body, (n_dp, n_c, feats, width, n_ck, n_...]
    unnamed x1, local copies, waits for them, and re-layouts: 1.87 us -> 0.8 us
where the time goes in v2:
time: 44.7 us; the launch traced here: 44.5 us
  Pallas kernels  43.7 us (98%)
  local copies, waits for them, and re-layouts  0.8 us (2%)
    pallas_call x1, Pallas kernels, on_device(): pl.pallas_call(functools.partial(body, (n_dp, n_c, feats, width, n_ck, n_...  43.7 us

profile of v2, /device:TPU:0, one launch (start us, length us, event | category | flops | bytes accessed | tf_op | source)
XLA Modules:
  0.0 44.5 jit_solution(16699500142499699341)
XLA Ops:
  0.0 43.7 %shard_map.37 = f32[64,2048]{1,0:T(8,128)S(1)} custom-call(bf16[32,4096]{1,0:T(8,128)(2,1)} %bitcast.5, bf16[32,2048]{1,0:T(8,128)(2,1)} %bitcast.7, bf16[64,2048]{1,0:T(8,128)(2,1)} %bitcast.6), custom_call_target="tpu_custom_call" | custom-call | tf_op jit(solution)/shard_map/pallas_call | solution.py:482
  43.7 0.8 %copy.5 = f32[2048,64]{0,1:T(8,128)} copy(f32[2048,64]{0,1:T(8,128)S(1)} %bitcast.4) | data formatting | bytes 1048576

commit v3 on v2

--- a/solution.py
+++ b/solution.py
@@ -10,15 +10,7 @@
 
 MESH = pl.DeviceIdType.MESH
 F32, BF16 = jnp.float32, jnp.bfloat16
-PIECE = 512
-
-
-def dot(a, b):
-    return lax.dot_general(a, b, (((1,), (0,)), ((), ())), preferred_element_type=F32)
-
-
-def dot_nt(a, b):
-    return lax.dot_general(a, b, (((1,), (1,)), ((), ())), preferred_element_type=F32)
+PIECE = 1024
 
 
 def split3(v):
@@ -59,22 +51,75 @@
     return out
 
 
-def staggered(pieces, lag=1):
-    held = []
-    for logits, apply in pieces:
-        e = logits()
-        if len(held) == lag:
-            tile, use = held.pop(0)
-            use(tile)
-        held.append((jnp.exp2(e).astype(BF16), apply))
-    for tile, use in held:
-        use(tile)
-
-
-def body(cfg, pts_hbm, cen_hbm, coef_hbm, out, pts, packed, lsem, sibp, kmat, colt, gath, reg, own_half, snd1, rcv1, snd2, rcv2,
-         own_sum, fwd, csend, crecv, cown, full, rowp, loc,
+class Mxu:
+    def __init__(self, q, tiles, sums):
+        self.q, self.tiles, self.sums, self.count = q, tiles, sums, 0
+
+    def push(self, value, transpose=False):
+        r = self.count % 2
+        self.count += 1
+        pltpu.matmul_push_rhs(value, staging_register=r, mxu_index=self.q, transpose=transpose)
+        return r
+
+    def stream(self, pairs, transpose):
+        made = 0
+        prev = []
+
+        def use(item, r):
+            pltpu.matmul_acc_lhs(self.sums[item[1][2]], item[1][3](), load_staged_rhs=r)
+
+        def tile(item):
+            value = jnp.exp2(pltpu.matmul_pop(self.tiles[item[0]])).astype(BF16)
+            item[1][1](value)
+            return self.push(value, transpose)
+
+        r = self.push(pairs[0][0]())
+        for i, (_, units) in enumerate(pairs):
+            now = []
+            for n in range(max(len(units), len(prev))):
+                if n < len(units):
+                    pltpu.matmul_acc_lhs(self.tiles[made % 3], units[n][0](), load_staged_rhs=r if n == 0 else None)
+                    now.append((made % 3, units[n]))
+                    made += 1
+                    yield
+                if n < len(prev):
+                    prev[n] = prev[n] + (tile(prev[n]),)
+                    yield
+            for n, item in enumerate(prev):
+                use(item, item[2])
+                if n == 0 and i + 1 < len(pairs):
+                    r = self.push(pairs[i + 1][0]())
+                yield
+            if not prev and i + 1 < len(pairs):
+                r = self.push(pairs[i + 1][0]())
+            prev = now
+        prev = [item + (tile(item),) for item in prev]
+        yield
+        for item in prev:
+            use(item, item[2])
+
+    def chain(self, items):
+        r = self.push(items[0][0]())
+        for n, (_, rows, k) in enumerate(items):
+            after = self.push(items[n + 1][0]()) if n + 1 < len(items) else None
+            pltpu.matmul_acc_lhs(self.sums[k], rows(), load_staged_rhs=r)
+            r = after
+            yield
+
+
+def together(streams):
+    streams = list(streams)
+    while streams:
+        for stream in list(streams):
+            if next(stream, streams) is streams:
+                streams.remove(stream)
+
+
+def inner(cfg, accs, pts_hbm, cen_hbm, coef_hbm, out, pts, packed, lsem, sibp, kmat, colt, gath, reg, own_half, snd1, rcv1, snd2, rcv2,
+         own_sum, fwd, csend, crecv, cown, full, rowp, rowg, loc,
          os_, or_, b1s, b1r, b2s, b2r, gs, gr, hs, hr, ups, upr, dns, dnr, fus, fur, fds, fdr, cs, cr, ds_, dr):
     n_dp, n_c, feats, width, n_ck, n_cc = cfg
+    mxu = [Mxu(q, accs[7 * q:7 * q + 3], accs[7 * q + 3:7 * q + 7]) for q in range(2)]
     n_h = n_c // 2
     d = lax.axis_index("dp")
     j = lax.axis_index("centers")
@@ -116,7 +161,9 @@
     cen_in.wait()
     for c in range(local_cen // piece):
         at = pl.ds(c * piece, piece)
-        colt[:, at] = col_form(packed[:feats, at], width)
+        colt[:width, at] = col_form(packed[:feats, at], width)
+    colt[width:, :] = jnp.zeros_like(colt[width:, :])
+    rowp[:, :, :, width:] = jnp.zeros_like(rowp[:, :, :, width:])
     reg[...] = jnp.zeros_like(reg)
     loc[...] = jnp.zeros_like(loc)
     coef_in.wait()
@@ -248,33 +295,44 @@
         for i, s in enumerate(range(g * group, (g + 1) * group)):
             for h, q in enumerate(owners(s)):
                 src = pl.ds(pl.multiple_of(q * share + (s // n_h) * sh, sh), sh)
-                rowp[g % 2, i, h * sh:(h + 1) * sh, :] = row_form(pts[:, src], width)
+                rowp[g % 2, i, h * sh:(h + 1) * sh, :width] = row_form(pts[:, src], width)
 
     def forward(g):
         if (g + 1) * group < steps:
             point_rows(g + 1)
-        pieces = []
-        accs = []
+        blocks = []
         for i, s in enumerate(range(g * group, (g + 1) * group)):
-            acc = [jnp.zeros((outs, 2 * sh), F32)]
-            accs.append(acc)
             ats = [pl.ds(pl.multiple_of((s // n_h) * span + q * sh, sh), sh) for q in owners(s)]
-            for b in range(local_cen // piece):
-                cols = pl.ds(b * piece, piece)
-
-                def logits(i=i, cols=cols):
-                    return dot(rowp[g % 2, i], colt[:, cols])
-
-                def apply(tile, acc=acc, ats=ats, cols=cols):
-                    for h in range(2):
-                        kmat[ats[h], cols] = tile[h * sh:(h + 1) * sh]
-                    acc[0] = acc[0] + dot_nt(packed[feats:, cols], tile)
-
-                pieces.append((logits, apply))
-        staggered(pieces)
-        for acc, s in zip(accs, range(g * group, (g + 1) * group)):
-            snd1[s] = acc[0][:, :sh].astype(BF16)
-            own_half[s] = acc[0][:, sh:]
+            for r in range(0, 2 * sh, 256):
+                held = [(ats[h], h * sh - r) for h in range(2) if r <= h * sh < r + 256]
+                blocks.append((s, i, r, held))
+        plans = []
+        for q in range(2):
+            pairs = []
+            for c in range(0, local_cen, 256):
+                cols = pl.ds(c, 256)
+                units = []
+                for n, (s, i, r, held) in enumerate(blocks[q::2]):
+
+                    def keep(tile, cols=cols, held=held):
+                        for at, o in held:
+                            kmat[at, cols] = tile[o:o + sh]
+
+                    units.append((
+                        lambda i=i, r=r: rowp[g % 2, i, r:r + 256, :], keep, n,
+                        lambda cols=cols: packed[feats:, cols],
+                    ))
+                pairs.append((lambda cols=cols: colt[:, cols], units))
+            plans.append(pairs)
+        together(mxu[q].stream(plans[q], True) for q in range(2))
+        for q in range(2):
+            for n, (s, i, r, held) in enumerate(blocks[q::2]):
+                total = pltpu.matmul_pop(mxu[q].sums[n])
+                for at, o in held:
+                    if r + o == 0:
+                        snd1[s] = total[:, o:o + sh].astype(BF16)
+                    else:
+                        own_half[s] = total[:, o:o + sh]
 
     def combine(s):
         c, k = s // n_h, n_h - 1 - s % n_h
@@ -303,27 +361,34 @@
             relay(c, k).start()
 
     def regular(*blocks):
-        pieces = []
-        for block in blocks:
-            rows = row_form(gath[block, :feats, :], width)
-            weights = gath[block, feats:, :]
-            for r in range(0, quarter, 256):
-                part = slice(r, r + 256)
-                for b in range(local_cen // piece):
-                    cols = pl.ds(b * piece, piece)
-
-                    def logits(rows=rows[part], cols=cols):
-                        return dot(rows, colt[:, cols])
-
-                    def apply(tile, weights=weights[:, part], cols=cols):
-                        reg[:, cols] += dot(weights, tile)
-
-                    pieces.append((logits, apply))
-        staggered(pieces, 2)
-
-    def back(c, at):
-        rows = pl.ds(c * span, span)
-        return dot(fwd[:, rows], kmat[rows, at]) * alpha_scale
+        for i, block in enumerate(blocks):
+            rowg[pl.ds(i * quarter, quarter), :width] = row_form(gath[block, :feats, :], width)
+        plans = []
+        for q in range(2):
+            pairs = []
+            for n, c in enumerate(range(q * 256, local_cen, 512)):
+                cols = pl.ds(c, 256)
+                for i, block in enumerate(blocks):
+                    units = [(
+                        lambda i=i, r=r: rowg[pl.ds(i * quarter + r, 256), :], lambda tile: None, n,
+                        lambda block=block, r=r: gath[block, feats:, pl.ds(r, 256)],
+                    ) for r in range(0, quarter, 256)]
+                    pairs.append((lambda cols=cols: colt[:, cols], units))
+            plans.append(pairs)
+        together(mxu[q].stream(plans[q], False) for q in range(2))
+        for q in range(2):
+            for n, c in enumerate(range(q * 256, local_cen, 512)):
+                reg[:, pl.ds(c, 256)] += pltpu.matmul_pop(mxu[q].sums[n])
+
+    def back(c, cols):
+        plans = []
+        for q in range(2):
+            plans.append([(
+                lambda k=k, at=at: kmat[pl.ds(c * span + k * 256, 256), at],
+                lambda k=k: fwd[:, pl.ds(c * span + k * 256, 256)], n,
+            ) for n, at in enumerate(cols[q::2]) for k in range(span // 256)])
+        together(mxu[q].chain(plans[q]) for q in range(2) if plans[q])
+        return [pltpu.matmul_pop(mxu[i % 2].sums[i // 2]) * alpha_scale for i in range(len(cols))]
 
     hops = list(range(1, n_h))
     sib_hops = list(range(1, n_h))
@@ -340,20 +405,23 @@
     own_cols = pl.ds(pl.multiple_of(d * quarter, 128), quarter)
 
     def local(src):
-        total = [loc[...]]
-        pieces = []
-        for b in range(local_cen // piece):
-            at = pl.ds(b * piece, piece)
-
-            def logits(at=at):
-                return dot(row_form(src[:feats, at], width), colt[:, own_cols])
-
-            def apply(tile, at=at):
-                total[0] = total[0] + dot(src[feats:, at], tile)
-
-            pieces.append((logits, apply))
-        staggered(pieces)
-        loc[...] = total[0]
+        rowg[:, :width] = row_form(src[:feats, :], width)
+        n_rows = local_cen // 256
+        plans = []
+        for q in range(2):
+            pairs = []
+            for n, c in enumerate(range(0, quarter, 256)):
+                cols = pl.ds(pl.multiple_of(d * quarter + c, 128), 256)
+                for b in range(q, n_rows, 4):
+                    units = [(
+                        lambda r=r: rowg[pl.ds(r * 256, 256), :], lambda tile: None, n,
+                        lambda r=r: src[feats:, pl.ds(r * 256, 256)],
+                    ) for r in range(b, min(b + 4, n_rows), 2)]
+                    pairs.append((lambda cols=cols: colt[:, cols], units))
+            plans.append(pairs)
+        together(mxu[q].stream(plans[q], False) for q in range(2))
+        for n, c in enumerate(range(0, quarter, 256)):
+            loc[:, c:c + 256] += pltpu.matmul_pop(mxu[0].sums[n]) + pltpu.matmul_pop(mxu[1].sums[n])
 
     last = n_ck - 1
     groups = steps // group
@@ -361,6 +429,7 @@
     for g in range(groups):
         forward(g)
         if g == 0:
+            rowg[:, width:] = jnp.zeros_like(rowg[:, width:])
             pl.semaphore_wait(barrier, n_h - 1 + 1 + n_dp - 1)
         for s in range(g * group, (g + 1) * group):
             to_sib(s).start()
@@ -380,11 +449,8 @@
     if n_ck > 1:
         finish(0)
     regular(near + 1 - par)
-    local(packed)
     ensure(2)
     finish(last)
-    own_to_sib.wait_recv()
-    local(sibp)
     rest = list(range(2, n_h))
     for k in rest[:-1]:
         ensure(k)
@@ -393,11 +459,13 @@
         regular(2 * xor(z, k) + 1 - par)
     if n_ck > 1:
         relays(0)
+        for k in rest[-1:]:
+            ensure(k)
         for k in range(n_h):
             relay_in(0, k).wait_recv()
-        for b in range(local_cen // piece):
-            cols = pl.ds(b * piece, piece)
-            reg[:, cols] += back(0, cols)
+        cols = [pl.ds(b, 256) for b in range(0, local_cen, 256)]
+        for at, value in zip(cols, back(0, cols)):
+            reg[:, at] += value
     for k in rest[-1:]:
         ensure(k)
         relays(last)
@@ -413,15 +481,22 @@
         return copy(csend.at[i], crecv.at[i], cs.at[i], cr.at[i], (xor(d, k), j))
 
     for cc in range(n_cc):
-        for k in reversed(range(n_dp)):
-            at = pl.ds(pl.multiple_of(xor(d, k) * quarter + cc * cw, 128), cw)
-            total = back(last, at) + reg[:, at]
-            if k > 0:
-                csend[cc * n_dp + k] = total
-            else:
-                cown[cc] = total + loc[:, cc * cw:(cc + 1) * cw]
-        for k in reversed(range(1, n_dp)):
-            cross(cc, k).start()
+        for first in range(n_dp - 1, -1, -2):
+            order = [first, first - 1]
+            ats = [pl.ds(pl.multiple_of(xor(d, k) * quarter + cc * cw, 128), cw) for k in order]
+            for k, at, value in zip(order, ats, back(last, ats)):
+                total = value + reg[:, at]
+                if k > 0:
+                    csend[cc * n_dp + k] = total
+                else:
+                    cown[cc] = total
+            for k in order:
+                if k > 0:
+                    cross(cc, k).start()
+
+    local(packed)
+    own_to_sib.wait_recv()
+    local(sibp)
 
     def publish(cc, k):
         i = cc * n_dp + k
@@ -436,7 +511,7 @@
     for cc in range(n_cc):
         for k in range(1, n_dp):
             cross(cc, k).wait_recv()
-        total = cown[cc]
+        total = cown[cc] + loc[:, cc * cw:(cc + 1) * cw]
         for k in range(1, n_dp):
             total = total + crecv[cc * n_dp + k]
         full[cc, d] = total
@@ -465,6 +540,16 @@
             publish(cc, k).wait_send()
 
 
+def body(cfg, *refs):
+    def run(*accs):
+        inner(cfg, accs, *refs)
+
+    specs = []
+    for q in range(2):
+        specs += [pltpu.ACC(q)((256, 256), F32)] * 3 + [pltpu.ACC(q)((64, 256), F32)] * 4
+    pl.run_scoped(run, *specs)
+
+
 def solution(mesh):
     n_dp, n_c = mesh.shape["dp"], mesh.shape["centers"]
 
@@ -475,7 +560,7 @@
         n_h = n_c // 2
         share, quarter = local_pts // n_c, local_cen // n_dp
         n_ck = 2 if share % 256 == 0 else 1
-        n_cc = 2 if quarter % 256 == 0 else 1
+        n_cc = quarter // 256
         sh, cw = share // n_ck, quarter // n_cc
         dma = pltpu.SemaphoreType.DMA
         args = [pltpu.with_memory_space_constraint(v.T, pltpu.HBM) for v in (points, centers, coef)]
@@ -490,7 +575,7 @@
                 dma((3,)),
                 pltpu.VMEM((feats + outs, local_cen), BF16),
                 pltpu.VMEM((local_pts, local_cen), BF16),
-                pltpu.VMEM((width, local_cen), BF16),
+                pltpu.VMEM((256, local_cen), BF16),
                 pltpu.VMEM((n_c, feats + outs, quarter), BF16),
                 pltpu.VMEM((outs, local_cen), F32),
                 pltpu.VMEM((n_ck * n_h, outs, sh), F32),
@@ -504,7 +589,8 @@
                 pltpu.VMEM((n_cc * n_dp, outs, cw), F32),
                 pltpu.VMEM((n_cc, outs, cw), F32),
                 pltpu.VMEM((n_cc, n_dp, outs, cw), F32),
-                pltpu.VMEM((2, 2, 2 * sh, width), BF16),
+                pltpu.VMEM((2, 2, 2 * sh, 256), BF16),
+                pltpu.VMEM((local_cen, 256), BF16),
                 pltpu.VMEM((outs, quarter), F32),
             ] + [dma((1,))] * 2 + [dma((n_ck * n_h,))] * 8 + [dma((n_h,))] * 8 + [dma((n_cc * n_dp,))] * 4,
             compiler_params=pltpu.CompilerParams(

time: 44.7 us -> 43.6 us (0.975)
  Pallas kernels: 43.7 us -> 42.6 us
    pallas_call x1, Pallas kernels: 43.7 us -> 42.6 us  [on_device(): pl.pallas_call(functools.partial(body, (n_dp, n_c, feats, width, n_ck, n_...]
where the time goes in v3:
time: 43.6 us; the launch traced here: 43.4 us
  Pallas kernels  42.6 us (98%)
  local copies, waits for them, and re-layouts  0.8 us (2%)
    pallas_call x1, Pallas kernels, on_device(): pl.pallas_call(functools.partial(body, (n_dp, n_c, feats, width, n_ck, n_...  42.6 us

profile of v3, /device:TPU:0, one launch (start us, length us, event | category | flops | bytes accessed | tf_op | source)
XLA Modules:
  0.0 43.4 jit_solution(15448889997428842654)
XLA Ops:
  0.0 42.6 %shard_map.37 = f32[64,2048]{1,0:T(8,128)S(1)} custom-call(bf16[32,4096]{1,0:T(8,128)(2,1)} %bitcast.5, bf16[32,2048]{1,0:T(8,128)(2,1)} %bitcast.7, bf16[64,2048]{1,0:T(8,128)(2,1)} %bitcast.6), custom_call_target="tpu_custom_call" | custom-call | tf_op jit(solution)/shard_map/pallas_call | solution.py:567
  42.6 0.8 %copy.5 = f32[2048,64]{0,1:T(8,128)} copy(f32[2048,64]{0,1:T(8,128)S(1)} %bitcast.4) | data formatting | bytes 1048576

commit v4 on v3

--- a/solution.py
+++ b/solution.py
@@ -425,20 +425,19 @@
 
     last = n_ck - 1
     groups = steps // group
+    pl.semaphore_wait(barrier, n_h - 1 + 1 + n_dp - 1)
+    hop(0)
     point_rows(0)
     for g in range(groups):
         forward(g)
         if g == 0:
             rowg[:, width:] = jnp.zeros_like(rowg[:, width:])
-            pl.semaphore_wait(barrier, n_h - 1 + 1 + n_dp - 1)
         for s in range(g * group, (g + 1) * group):
             to_sib(s).start()
-        if g == 0:
-            hop(0)
         if g > 0:
             for s in range((g - 1) * group, g * group):
                 combine(s)
-        if g == groups - 2:
+        if g == max(groups - 3, 0):
             ensure(1)
             own_to_sib.start()
     near = 2 * xor(z, 1)
@@ -448,8 +447,8 @@
         combine(s)
     if n_ck > 1:
         finish(0)
+    ensure(2)
     regular(near + 1 - par)
-    ensure(2)
     finish(last)
     rest = list(range(2, n_h))
     for k in rest[:-1]:

time: 43.6 us -> 43.7 us (level)
  no operation moved by 1% of the time
where the time goes in v4:
time: 43.7 us; the launch traced here: 43.6 us
  Pallas kernels  42.8 us (98%)
  local copies, waits for them, and re-layouts  0.8 us (2%)
    pallas_call x1, Pallas kernels, on_device(): pl.pallas_call(functools.partial(body, (n_dp, n_c, feats, width, n_ck, n_...  42.8 us

profile of v4, /device:TPU:0, one launch (start us, length us, event | category | flops | bytes accessed | tf_op | source)
XLA Modules:
  0.0 43.6 jit_solution(6946740393410280954)
XLA Ops:
  0.0 42.8 %shard_map.37 = f32[64,2048]{1,0:T(8,128)S(1)} custom-call(bf16[32,4096]{1,0:T(8,128)(2,1)} %bitcast.5, bf16[32,2048]{1,0:T(8,128)(2,1)} %bitcast.7, bf16[64,2048]{1,0:T(8,128)(2,1)} %bitcast.6), custom_call_target="tpu_custom_call" | custom-call | tf_op jit(solution)/shard_map/pallas_call | solution.py:566
  42.8 0.8 %copy.5 = f32[2048,64]{0,1:T(8,128)} copy(f32[2048,64]{0,1:T(8,128)S(1)} %bitcast.4) | data formatting | bytes 1048576
